TPU v7x, 256 devices: a 8x8x2 block of a 8x8x16 slice. The times are simulated.
256 devices in a mesh: groups: 2 (over z), seq: 16 (over y, core), head: 8 (over x).
Axes of the slice: x: 8, y: 8, z: 2, core: 2. Of those that a mesh axis runs over, the one named last changes fastest.
The devices are a block of a 8x8x16 slice.
Arguments:
- queries: bfloat16 [4096, 8192], P(('groups', 'seq'), 'head'), parts along dimension 0
- new_keys: bfloat16 [4096, 1024], P(('groups', 'seq'), 'head'), parts along dimension 0, may hold values from -6 to 6
- new_values: bfloat16 [4096, 1024], P(('groups', 'seq'), 'head'), parts along dimension 0, may hold values from -6 to 6
- cache_keys: bfloat16 [32768, 1024], P(('groups', 'seq'), 'head'), parts along dimension 0
- cache_values: bfloat16 [32768, 1024], P(('groups', 'seq'), 'head'), parts along dimension 0, may hold values from -6 to 6
- valid_len: int32 [32], P('groups'), parts along dimension 0, may hold values from 1 to 1024, as said below
- block_of: int32 [32], P('groups'), parts along dimension 0, may hold values from 0 to 15, each once
Outputs:
- attended: bfloat16 [4096, 8192], P(('groups', 'seq'), 'head'), parts along dimension 0
There are 2 independent parts, one for each index of `groups`. A program takes and returns all parts, laid end to end along the dimension named above; each array names one. Nothing has to cross between parts.
Inputs may be any that keep to these rules, and one draw needn't show every extreme that they name: `valid_len`: some shard is full (1024 filled slots) in every draw; slot 0 of every shard is filled. `block_of`: A permutation of the 16 span blocks.
All inputs are finite; a program needn't handle non-finite values.
Results may differ from a plain program's by a relative error of at most 0.0027.
Values may be sent and summed in bfloat16 or wider, within the bound.
No kernel may reach another device: no remote copies, remote signals or barrier semaphores. Data moves between devices by JAX's collectives and lax.ppermute only.
A program may use at most 192 MiB of HBM per device.

v0:
```python
import jax
import jax.numpy as jnp
from jax import lax
from jax.sharding import PartitionSpec as P

DH = 128
GROUP = 8
NEGATIVE = -1e30


def in_order(tiles, dim):
    shape = list(tiles.shape[1:])
    shape[dim] *= tiles.shape[0]
    return jnp.moveaxis(tiles, 0, dim).reshape(shape)


def from_everyone(array, axis):
    size = lax.axis_size(axis)
    return lax.all_to_all(
        jnp.broadcast_to(array[None], (size, *array.shape)), axis, 0, 0, tiled=True
    )


def gather_directly(array, axis, dim):
    return in_order(from_everyone(array, axis), dim)


def sent_together(arrays, axis, dim, along):
    both = jnp.concatenate(arrays, axis=along)
    filled, at, done = (gather_directly(both, axis, dim), 0, [])
    for a in arrays:
        done.append(lax.slice_in_dim(filled, at, at + a.shape[along], axis=along))
        at += a.shape[along]
    return tuple(done)


def lookup(table, where_at):
    picked = where_at[:, None] == jnp.arange(table.shape[0], dtype=jnp.int32)[None, :]
    return jnp.sum(jnp.where(picked, table[None, :], 0), axis=1)


def scores_of(query_rows, key_rows):
    heads = key_rows.shape[1] // DH
    query_four = query_rows.reshape(query_rows.shape[0], heads, GROUP, DH)
    key_three = key_rows.reshape(key_rows.shape[0], heads, DH)
    product = jnp.einsum(
        "rkgd,nkd->rkgn", query_four, key_three, preferred_element_type=jnp.float32
    )
    return product * DH ** (-0.5)


def visible(query_pos, key_pos, key_live):
    return (key_live[None, :] & (key_pos[None, :] <= query_pos[:, None]))[:, None, None, :]


def masked_max(scores, seen):
    return jnp.max(jnp.where(seen, scores, NEGATIVE), axis=-1)


def weights_of(scores, seen, top):
    return jnp.where(seen, jnp.exp(scores - top[..., None]), 0.0)


def accumulate(weights, value_rows):
    heads = value_rows.shape[1] // DH
    value_three = value_rows.reshape(value_rows.shape[0], heads, DH)
    return jnp.einsum(
        "rkgn,nkd->rkgd",
        weights.astype(jnp.bfloat16),
        value_three,
        preferred_element_type=jnp.float32,
    )


def on_device(queries, new_keys, new_values, cache_keys, cache_values, valid_len, block_of):
    here = jnp.reshape(lax.axis_index("seq"), (1,))
    rows_here = queries.shape[0]
    length = cache_keys.shape[0]
    heads = new_keys.shape[1] // DH
    own_block = lookup(block_of, here)[0]
    span_k, span_v = sent_together((new_keys, new_values), "seq", 0, 1)
    total = span_k.shape[0]
    every = jnp.arange(total, dtype=jnp.int32)
    span_pos = lookup(block_of, every // rows_here) * rows_here + every % rows_here
    own_pos = own_block * rows_here + jnp.arange(rows_here, dtype=jnp.int32)
    start_state = (
        jnp.full((rows_here, heads, GROUP), NEGATIVE, jnp.float32),
        jnp.zeros((rows_here, heads, GROUP, DH), jnp.float32),
        jnp.zeros((rows_here, heads, GROUP), jnp.float32),
    )
    pieces = (
        lax.all_gather(cache_keys, "seq", axis=0, tiled=True),
        lax.all_gather(cache_values, "seq", axis=0, tiled=True),
    )
    count = pieces[0].shape[0]
    many = count // length

    def inner(state, item):
        key_block, value_block, first = item
        shard = first // length
        block_k = lax.dynamic_slice_in_dim(span_k, shard * rows_here, rows_here, 0)
        block_v = lax.dynamic_slice_in_dim(span_v, shard * rows_here, rows_here, 0)
        block_pos = lax.dynamic_slice_in_dim(span_pos, shard * rows_here, rows_here, 0)
        filled = lookup(valid_len, jnp.reshape(shard, (1,)))[0]
        cache_live = jnp.arange(length, dtype=jnp.int32) < filled
        cache_seen = jnp.broadcast_to(cache_live[None, None, None, :], (rows_here, 1, 1, length))
        block_seen = visible(own_pos, block_pos, jnp.ones((rows_here,), bool))
        seen = jnp.concatenate([cache_seen, block_seen], -1)
        keys = jnp.concatenate([key_block, block_k], 0)
        values = jnp.concatenate([value_block, block_v], 0)
        scores = scores_of(queries, keys)
        local = masked_max(scores, seen)
        weights = weights_of(scores, seen, local)
        part_numer = accumulate(weights, values)
        part_total = jnp.sum(weights, axis=-1)
        best, sums, totals = state
        newest = jnp.maximum(best, local)
        keep = jnp.exp(best - newest)
        fresh = jnp.exp(local - newest)
        sums = sums * keep[..., None] + part_numer * fresh[..., None]
        totals = totals * keep + part_total * fresh
        return ((newest, sums, totals), None)

    firsts = length * jnp.arange(many, dtype=jnp.int32)
    state, _ = lax.scan(
        inner,
        start_state,
        (pieces[0].reshape(many, length, -1), pieces[1].reshape(many, length, -1), firsts),
    )
    final_top, numer, denom = state
    result = numer / denom[..., None]
    return result.reshape(rows_here, -1).astype(jnp.bfloat16)


def solution(mesh):
    placed = (
        P(("groups", "seq"), "head"),
        P(("groups", "seq"), "head"),
        P(("groups", "seq"), "head"),
        P(("groups", "seq"), "head"),
        P(("groups", "seq"), "head"),
        P("groups"),
        P("groups"),
    )
    return jax.shard_map(
        on_device,
        mesh=mesh,
        in_specs=placed,
        out_specs=P(("groups", "seq"), "head"),
        check_vma=False,
    )
```

profile of v0, /device:TPU:513, one launch (start us, length us, event | category | flops | bytes accessed | tf_op | source)
XLA Modules:
  0.0 292.7 jit_solution(12681562831767876139)
XLA Ops:
  9.0 1.3 broadcast_in_dim.92
  10.3 23.9 %all-to-all-start = ((bf16[16,128,256]{1,2,0:T(8,128)(2,1)}), bf16[16,128,256]{1,2,0:T(8,128)(2,1)S(1)}, u32[]{:S(2)}, u32[]{:S(2)}) async-start(bf16[16,128,256]{1,2,0:T(8,128)(2,1)} %broadcast_in_dim.92), calls=%async_computation | async-start | bytes 2097152 | tf_op jit(solution)/shard_map/all_to_all | solution.py:19
  34.2 1.4 fusion.47
  37.0 32.5 %all-to-all-done = bf16[16,128,256]{1,2,0:T(8,128)(2,1)S(1)} async-done(((bf16[16,128,256]{1,2,0:T(8,128)(2,1)}), bf16[16,128,256]{1,2,0:T(8,128)(2,1)S(1)}, u32[]{:S(2)}, u32[]{:S(2)}) %all-to-all-start) | async-done | bytes 1048608 | tf_op jit(solution)/shard_map/all_to_all | solution.py:19
  70.1 15.4 %all-gather.3.cloned.1.call-done = bf16[16384,128]{1,0:T(8,128)(2,1)} async-done(((bf16[1024,128]{1,0:T(8,128)(2,1)}), bf16[16384,128]{1,0:T(8,128)(2,1)}) %all-gather.3.cloned.1.call-update) | async-done | bytes 4194320 | tf_op jit(solution)/shard_map/all_gather | solution.py:92
  85.5 45.5 %all-gather.5.cloned.1.call-done = bf16[16384,128]{1,0:T(8,128)(2,1)} async-done(((bf16[1024,128]{1,0:T(8,128)(2,1)}), bf16[16384,128]{1,0:T(8,128)(2,1)}) %all-gather.5.cloned.1.call-update) | async-done | bytes 4194320 | tf_op jit(solution)/shard_map/all_gather | solution.py:93
  131.0 153.9 %while.17 = (s32[]{:T(128)}, f32[128,1,8]{0,2,1:T(8,128)S(1)}, f32[128,1,8,128]{0,3,2,1:T(8,128)S(1)}, f32[128,1,8]{0,2,1:T(8,128)S(1)}, s32[16]{0:T(128)S(1)}, ...) while((s32[]{:T(128)}, f32[128,1,8]{0,2,1:T(8,128)S(1)}, ...), condition=%wide.region_6.7_spmd.clone, body=%wide.region_2.6_spmd.clone.sunk | while | flops 616474816 | bytes 18533632 | solution.py:125
  139.5 1.1 fusion.65
  149.2 1.1 fusion.65
  155.0 1.0 constant_dynamic-slice_fusion.6
  156.1 1.0 dynamic-slice_bitcast_fusion.2
  158.8 1.1 fusion.65
  164.6 1.0 constant_dynamic-slice_fusion.6
  165.7 1.0 dynamic-slice_bitcast_fusion.2
  168.4 1.1 fusion.65
  174.2 1.0 constant_dynamic-slice_fusion.6
  175.3 1.0 dynamic-slice_bitcast_fusion.2
  178.0 1.1 fusion.65
  183.8 1.0 constant_dynamic-slice_fusion.6
  185.0 1.0 dynamic-slice_bitcast_fusion.2
  187.6 1.1 fusion.65
  197.3 1.1 fusion.65
  206.9 1.1 fusion.65
  213.8 1.0 dynamic-slice_bitcast_fusion.2
  216.5 1.1 fusion.65
  226.1 1.1 fusion.65
  235.8 1.1 fusion.65
  245.4 1.1 fusion.65
  255.0 1.1 fusion.65
  264.6 1.1 fusion.65
  274.2 1.1 fusion.65
  283.9 1.1 fusion.65
  (300 shorter events, 93.3 us)
Async XLA Ops:
  6.5 124.5 %copy-start.1 = (s32[16]{0:T(128)S(1)}, s32[16]{0:T(128)}, u32[]{:S(2)}) copy-start(s32[16]{0:T(128)} %param.14) | copy-start | bytes 196
  6.5 124.5 %copy-start = (bf16[128,1024]{1,0:T(8,128)(2,1)S(1)}, bf16[128,1024]{1,0:T(8,128)(2,1)}, u32[]{:S(2)}) copy-start(bf16[128,1024]{1,0:T(8,128)(2,1)} %param.9) | copy-start | bytes 786436
  6.6 78.9 %all-gather.3.cloned.1.call-start = ((), (), s32[]{:S(2)}) async-start(), calls=%async_computation.1 | async-start | bytes 4456448 | tf_op jit(solution)/shard_map/all_gather | solution.py:92
  7.3 123.7 %all-gather.5.cloned.1.call-start = ((), (), s32[]{:S(2)}) async-start(), calls=%async_computation.2 | async-start | bytes 4456448 | tf_op jit(solution)/shard_map/all_gather | solution.py:93
  10.3 59.2 %all-to-all-start = ((bf16[16,128,256]{1,2,0:T(8,128)(2,1)}), bf16[16,128,256]{1,2,0:T(8,128)(2,1)S(1)}, u32[]{:S(2)}, u32[]{:S(2)}) async-start(bf16[16,128,256]{1,2,0:T(8,128)(2,1)} %broadcast_in_dim.92), calls=%async_computation | async-start | bytes 2097152 | tf_op jit(solution)/shard_map/all_to_all | solution.py:19
Sparse Core Ops, SparseCore 0:
  9.2 76.2 all-gather.2
  87.3 43.6 all-gather.4
where the time goes:
time: 295 us; the launch traced here: 293 us
  waiting for transfers between devices  94.9 us (32%)
  local copies, waits for them, and re-layouts  49.1 us (17%)
  other arithmetic  40.9 us (14%)
  loops' own time  39 us (13%)
  matrix products  30.6 us (10%)
  starting transfers between devices  23.9 us (8%)
  between operations  14.2 us (5%)
    all_gather x1, waiting for transfers between devices, on_device(): lax.all_gather(cache_values, 'seq', axis=0, tiled=True)  45.5 us
    another operation x1, loops' own time, on_device(): lax.scan(inner, start_state, (pieces[0].reshape(many, length, -1), pieces...  39 us
    all_to_all x1, waiting for transfers between devices, from_everyone(): lax.all_to_all(jnp.broadcast_to(array[None], (size, *array.shape)), axis,...  32.5 us
    dynamic_slice x48, local copies, waits for them, and re-layouts, on_device(): lax.scan(inner, start_state, (pieces[0].reshape(many, length, -1), pieces...  27.4 us
    all_to_all x1, starting transfers between devices, from_everyone(): lax.all_to_all(jnp.broadcast_to(array[None], (size, *array.shape)), axis,...  23.9 us
    dot_general x16, matrix products, accumulate(): jnp.einsum('rkgn,nkd->rkgd', weights.astype(jnp.bfloat16), value_three, p...  17.5 us
    squeeze x16, local copies, waits for them, and re-layouts, on_device(): lax.scan(inner, start_state, (pieces[0].reshape(many, length, -1), pieces...  15.6 us
    all_gather x1, waiting for transfers between devices, on_device(): lax.all_gather(cache_keys, 'seq', axis=0, tiled=True)  15.4 us
  transfers between devices with their start and end apart: 3, of which 3 were waited for; matrix products, arithmetic and copies ran while one was open for 2% of the time, Pallas kernels for 0%

commit v1 on v0

--- a/solution.py
+++ b/solution.py
@@ -6,6 +6,11 @@
 DH = 128
 GROUP = 8
 NEGATIVE = -1e30
+
+
+def gather_over(x, axis, dim):
+    outgoing = jnp.stack([x] * lax.axis_size(axis))
+    return jnp.concatenate(lax.all_to_all(outgoing, axis, 0, 0), axis=dim)
 
 
 def in_order(tiles, dim):
@@ -89,7 +94,7 @@
         jnp.zeros((rows_here, heads, GROUP), jnp.float32),
     )
     pieces = (
-        lax.all_gather(cache_keys, "seq", axis=0, tiled=True),
+        gather_over(cache_keys, "seq", 0),
         lax.all_gather(cache_values, "seq", axis=0, tiled=True),
     )
     count = pieces[0].shape[0]

time: 295 us -> 335 us (1.14)
  waiting for transfers between devices: 94.9 us -> 128 us
  starting transfers between devices: 23.9 us -> 29.2 us
  local copies, waits for them, and re-layouts: 49.1 us -> 52.8 us
    all_to_all x0 -> x1, waiting for transfers between devices: none -> 60.7 us  [gather_over(): return jnp.concatenate(lax.all_to_all(outgoing, axis, 0, 0), axis=dim)]
    all_gather x1 -> x0, waiting for transfers between devices: 15.4 us -> none  [on_device(): lax.all_gather(cache_keys, 'seq', axis=0, tiled=True)]
    all_gather x1, waiting for transfers between devices: 45.5 us -> 36.9 us  [on_device(): lax.all_gather(cache_values, 'seq', axis=0, tiled=True)]
    all_to_all x0 -> x1, starting transfers between devices: none -> 5.27 us  [gather_over(): return jnp.concatenate(lax.all_to_all(outgoing, axis, 0, 0), axis=dim)]
    another operation x0 -> x1, local copies, waits for them, and re-layouts: none -> 3.72 us  [gather_over(): outgoing = jnp.stack([x] * lax.axis_size(axis))]
where the time goes in v1:
time: 335 us; the launch traced here: 333 us
  waiting for transfers between devices  128 us (38%)
  local copies, waits for them, and re-layouts  52.8 us (16%)
  other arithmetic  39.6 us (12%)
  loops' own time  39 us (12%)
  matrix products  30.6 us (9%)
  starting transfers between devices  29.2 us (9%)
  between operations  14.1 us (4%)
    all_to_all x1, waiting for transfers between devices, gather_over(): return jnp.concatenate(lax.all_to_all(outgoing, axis, 0, 0), axis=dim)  60.7 us
    another operation x1, loops' own time, on_device(): lax.scan(inner, start_state, (pieces[0].reshape(many, length, -1), pieces...  39 us
    all_gather x1, waiting for transfers between devices, on_device(): lax.all_gather(cache_values, 'seq', axis=0, tiled=True)  36.9 us
    all_to_all x1, waiting for transfers between devices, from_everyone(): lax.all_to_all(jnp.broadcast_to(array[None], (size, *array.shape)), axis,...  29.2 us
    dynamic_slice x48, local copies, waits for them, and re-layouts, on_device(): lax.scan(inner, start_state, (pieces[0].reshape(many, length, -1), pieces...  27.4 us
    all_to_all x1, starting transfers between devices, from_everyone(): lax.all_to_all(jnp.broadcast_to(array[None], (size, *array.shape)), axis,...  23.9 us
    dot_general x16, matrix products, accumulate(): jnp.einsum('rkgn,nkd->rkgd', weights.astype(jnp.bfloat16), value_three, p...  17.5 us
    squeeze x16, local copies, waits for them, and re-layouts, on_device(): lax.scan(inner, start_state, (pieces[0].reshape(many, length, -1), pieces...  15.6 us
  transfers between devices with their start and end apart: 3, of which 3 were waited for; matrix products, arithmetic and copies ran while one was open for 2% of the time, Pallas kernels for 0%

profile of v1, /device:TPU:513, one launch (start us, length us, event | category | flops | bytes accessed | tf_op | source)
XLA Modules:
  0.0 333.0 jit_solution(12316980330915372116)
XLA Ops:
  7.4 1.2 broadcast_in_dim.92
  8.6 23.9 %all-to-all-start.1 = ((bf16[16,128,256]{1,2,0:T(8,128)(2,1)}), bf16[16,128,256]{1,2,0:T(8,128)(2,1)S(1)}, u32[]{:S(2)}, u32[]{:S(2)}) async-start(bf16[16,128,256]{1,2,0:T(8,128)(2,1)} %broadcast_in_dim.92), calls=%async_computation.1 | async-start | bytes 2097152 | tf_op jit(solution)/shard_map/all_to_all | solution.py:24
  33.3 29.2 %all-to-all-done.1 = bf16[16,128,256]{1,2,0:T(8,128)(2,1)S(1)} async-done(((bf16[16,128,256]{1,2,0:T(8,128)(2,1)}), bf16[16,128,256]{1,2,0:T(8,128)(2,1)S(1)}, u32[]{:S(2)}, u32[]{:S(2)}) %all-to-all-start.1) | async-done | bytes 1048608 | tf_op jit(solution)/shard_map/all_to_all | solution.py:24
  62.5 3.7 %stack.2 = bf16[16,1024,128]{2,1,0:T(8,128)(2,1)} broadcast(bf16[1024,128]{1,0:T(8,128)(2,1)} %param.12), dimensions={1,2} | broadcast | bytes 4456448 | tf_op jit(solution)/shard_map/stack | solution.py:12
  66.2 5.3 %all-to-all-start = ((bf16[16,1024,128]{2,1,0:T(8,128)(2,1)}), bf16[16,1024,128]{2,1,0:T(8,128)(2,1)}, u32[]{:S(2)}, u32[]{:S(2)}) async-start(bf16[16,1024,128]{2,1,0:T(8,128)(2,1)} %stack.2), calls=%async_computation | async-start | bytes 8388608 | tf_op jit(solution)/shard_map/all_to_all | solution.py:13
  73.6 36.9 %all-gather.2.cloned.1.call-done = bf16[16384,128]{1,0:T(8,128)(2,1)} async-done(((bf16[1024,128]{1,0:T(8,128)(2,1)}), bf16[16384,128]{1,0:T(8,128)(2,1)}) %all-gather.2.cloned.1.call-update) | async-done | bytes 4194320 | tf_op jit(solution)/shard_map/all_gather | solution.py:98
  110.5 60.7 %all-to-all-done = bf16[16,1024,128]{2,1,0:T(8,128)(2,1)} async-done(((bf16[16,1024,128]{2,1,0:T(8,128)(2,1)}), bf16[16,1024,128]{2,1,0:T(8,128)(2,1)}, u32[]{:S(2)}, u32[]{:S(2)}) %all-to-all-start) | async-done | bytes 4194336 | tf_op jit(solution)/shard_map/all_to_all | solution.py:13
  171.3 153.9 %while.17 = (s32[]{:T(128)}, f32[128,1,8]{0,2,1:T(8,128)S(1)}, f32[128,1,8,128]{0,3,2,1:T(8,128)S(1)}, f32[128,1,8]{0,2,1:T(8,128)S(1)}, s32[16]{0:T(128)S(1)}, ...) while((s32[]{:T(128)}, f32[128,1,8]{0,2,1:T(8,128)S(1)}, ...), condition=%wide.region_6.7_spmd.clone, body=%wide.region_2.6_spmd.clone.sunk | while | flops 616474816 | bytes 18533632 | solution.py:130
  176.0 1.0 constant_dynamic-slice_fusion.6
  177.1 1.0 dynamic-slice_bitcast_fusion.2
  179.8 1.1 fusion.65
  189.4 1.1 fusion.65
  195.2 1.0 constant_dynamic-slice_fusion.6
  196.4 1.0 dynamic-slice_bitcast_fusion.2
  199.0 1.1 fusion.65
  208.7 1.1 fusion.65
  218.3 1.1 fusion.65
  224.1 1.0 constant_dynamic-slice_fusion.6
  225.2 1.0 dynamic-slice_bitcast_fusion.2
  227.9 1.1 fusion.65
  234.8 1.0 dynamic-slice_bitcast_fusion.2
  237.5 1.1 fusion.65
  243.3 1.0 constant_dynamic-slice_fusion.6
  247.1 1.1 fusion.65
  256.8 1.1 fusion.65
  266.4 1.1 fusion.65
  276.0 1.1 fusion.65
  285.6 1.1 fusion.65
  295.2 1.1 fusion.65
  304.9 1.1 fusion.65
  314.5 1.1 fusion.65
  324.1 1.1 fusion.65
  (302 shorter events, 93.6 us)
Async XLA Ops:
  8.6 53.9 %all-to-all-start.1 = ((bf16[16,128,256]{1,2,0:T(8,128)(2,1)}), bf16[16,128,256]{1,2,0:T(8,128)(2,1)S(1)}, u32[]{:S(2)}, u32[]{:S(2)}) async-start(bf16[16,128,256]{1,2,0:T(8,128)(2,1)} %broadcast_in_dim.92), calls=%async_computation.1 | async-start | bytes 2097152 | tf_op jit(solution)/shard_map/all_to_all | solution.py:24
  32.5 78.0 %all-gather.2.cloned.1.call-start = ((), (), s32[]{:S(2)}) async-start(), calls=%async_computation.2 | async-start | bytes 4456448 | tf_op jit(solution)/shard_map/all_gather | solution.py:98
  66.2 5.3 %copy-start = (s32[16]{0:T(128)S(1)}, s32[16]{0:T(128)}, u32[]{:S(2)}) copy-start(s32[16]{0:T(128)} %param.15) | copy-start | bytes 196
  66.2 105.0 %copy-start.1 = (bf16[128,1024]{1,0:T(8,128)(2,1)S(1)}, bf16[128,1024]{1,0:T(8,128)(2,1)}, u32[]{:S(2)}) copy-start(bf16[128,1024]{1,0:T(8,128)(2,1)} %param.9) | copy-start | bytes 786436
  66.2 105.0 %copy-start.2 = (s32[16]{0:T(128)S(1)}, s32[16]{0:T(128)}, u32[]{:S(2)}) copy-start(s32[16]{0:T(128)} %param.14) | copy-start | bytes 196
  66.2 105.0 %all-to-all-start = ((bf16[16,1024,128]{2,1,0:T(8,128)(2,1)}), bf16[16,1024,128]{2,1,0:T(8,128)(2,1)}, u32[]{:S(2)}, u32[]{:S(2)}) async-start(bf16[16,1024,128]{2,1,0:T(8,128)(2,1)} %stack.2), calls=%async_computation | async-start | bytes 8388608 | tf_op jit(solution)/shard_map/all_to_all | solution.py:13
Sparse Core Ops, SparseCore 0:
  35.2 75.3 all-gather.1
